TPU v7x, 32 devices: a whole 2x2x4 slice. The times are simulated.
32 devices in a mesh: nodes: 32 (over z, y, x, core).
Axes of the slice: x: 2, y: 2, z: 4, core: 2. Of those that a mesh axis runs over, the one named last changes fastest.
Arguments:
- adjacency: bfloat16 [16384, 16384], P('nodes')
- features: bfloat16 [16384, 128], P('nodes')
- w_one: float32 [128, 128], replicated
- w_two: float32 [128, 40], replicated
- labels: int32 [16384], P('nodes')
- label_mask: int32 [16384], P('nodes')
Outputs:
- output 1: float32 [1], replicated
- output 2: float32 [128, 128], replicated
- output 3: float32 [128, 40], replicated
All inputs are finite; a program needn't handle non-finite values.
Results may differ from a plain program's by a relative error of at most 0.001.
Values are sent between devices in bfloat16 or wider.
A program may use at most 1 GiB of HBM per device.

v0:
```python
import jax
import jax.numpy as jnp
from jax import lax
from jax.sharding import PartitionSpec as P

ROW_CONTRACT = (((0,), (0,)), ((), ()))
COL_CONTRACT = (((1,), (1,)), ((), ()))


def solution(mesh):
    axis_name = 'nodes'

    def local_step(adj_rows, feat_rows, w_one, w_two, label_rows, mask_rows):
        weight_one = w_one.astype(jnp.bfloat16)
        weight_two = w_two.astype(jnp.bfloat16)
        num_classes = w_two.shape[1]
        feats_all = lax.all_gather(feat_rows, axis_name, tiled=True)
        agg_one = jnp.dot(adj_rows, feats_all, preferred_element_type=jnp.float32).astype(jnp.bfloat16)
        pre_one = jnp.dot(agg_one, weight_one, preferred_element_type=jnp.float32)
        hidden = jnp.maximum(pre_one, 0.0).astype(jnp.bfloat16)
        hidden_all = lax.all_gather(hidden, axis_name, tiled=True)
        agg_two = jnp.dot(adj_rows, hidden_all, preferred_element_type=jnp.float32).astype(jnp.bfloat16)
        logits = jnp.dot(agg_two, weight_two, preferred_element_type=jnp.float32)
        weight = mask_rows.astype(jnp.float32)
        label_count = lax.psum(jnp.sum(weight), axis_name)
        onehot = (label_rows[:, None] == jnp.arange(num_classes)[None, :]).astype(jnp.float32)
        log_prob = jax.nn.log_softmax(logits, axis=-1)
        loss_sum = lax.psum(-jnp.sum(weight * jnp.sum(onehot * log_prob, axis=-1)), axis_name)
        grad_two = (weight[:, None] * (jnp.exp(log_prob) - onehot) / label_count).astype(jnp.bfloat16)
        dw_two = lax.psum(lax.dot_general(agg_two, grad_two, ROW_CONTRACT, preferred_element_type=jnp.float32), axis_name)
        back_two = lax.dot_general(grad_two, weight_two, COL_CONTRACT, preferred_element_type=jnp.float32).astype(jnp.bfloat16)
        part_sums = lax.dot_general(adj_rows, back_two, ROW_CONTRACT, preferred_element_type=jnp.float32)
        d_hidden = lax.psum_scatter(part_sums, axis_name, scatter_dimension=0, tiled=True)
        grad_one = jnp.where(pre_one > 0.0, d_hidden, 0.0).astype(jnp.bfloat16)
        dw_one = lax.psum(lax.dot_general(agg_one, grad_one, ROW_CONTRACT, preferred_element_type=jnp.float32), axis_name)
        return ((loss_sum / label_count).reshape(1), dw_one, dw_two)

    return jax.shard_map(local_step, mesh=mesh, in_specs=(P(axis_name, None), P(axis_name, None), P(None, None), P(None, None), P(axis_name), P(axis_name)), out_specs=(P(None), P(None, None), P(None, None)), check_vma=False)
```

profile of v0, /device:TPU:0, one launch (start us, length us, event | category | flops | bytes accessed | tf_op | source)
XLA Modules:
  0.0 501.1 jit_solution(2808808884760747712)
XLA Ops:
  7.2 0.0 copy-start.1
  7.2 0.0 copy-start.3
  7.2 0.0 all-gather.3.cloned.1.call-start
  7.2 0.7 all-gather.3.cloned.1.call-update
  7.9 0.0 copy-start
  7.9 0.0 copy-start.2
  7.9 0.0 all-gather.5.cloned.1.call-start
  8.0 67.7 %all-gather.3.cloned.1.call-done = bf16[16384,128]{1,0:T(8,128)(2,1)} async-done(((bf16[512,128]{1,0:T(8,128)(2,1)}), bf16[16384,128]{1,0:T(8,128)(2,1)}) %all-gather.3.cloned.1.call-update) | async-done | bytes 4194320 | tf_op jit(solution)/shard_map/all_gather | solution.py:17
  75.7 11.4 %convolution_convert_fusion.2 = bf16[512,128]{1,0:T(8,128)(2,1)S(1)} fusion(bf16[512,16384]{1,0:T(8,128)(2,1)} %param.6, bf16[16384,128]{1,0:T(8,128)(2,1)} %all-gather.3.cloned.1.call-done), kind=kOutput, calls=%fused_computation.3 | convolution fusion | flops 2147549184 | bytes 21102592 | tf_op jit(solution)/shard_map/dot_general | solution.py:18
  87.1 0.0 copy-done.1
  87.2 0.8 maximum_convert_fusion
  88.0 0.0 all-gather.5.cloned.1.call-update
  88.0 0.0 reduce-scatter.2.cloned.1.call-start
  88.1 0.0 copy-done.3
  88.1 60.6 %all-gather.5.cloned.1.call-done = bf16[16384,128]{1,0:T(8,128)(2,1)} async-done(((bf16[512,128]{1,0:T(8,128)(2,1)}), bf16[16384,128]{1,0:T(8,128)(2,1)}) %all-gather.5.cloned.1.call-update) | async-done | bytes 4194320 | tf_op jit(solution)/shard_map/all_gather | solution.py:21
  148.6 12.7 %convolution_convert_fusion.1 = bf16[128,512]{1,0:T(8,128)(2,1)S(1)} fusion(bf16[16384,128]{1,0:T(8,128)(2,1)} %all-gather.5.cloned.1.call-done, bf16[512,16384]{1,0:T(8,128)(2,1)} %param.6), kind=kOutput, calls=%fused_computation.2 | convolution fusion | flops 2147549184 | bytes 21102592 | tf_op jit(solution)/shard_map/dot_general | solution.py:22
  161.4 0.0 copy-done
  161.4 0.2 fusion.10
  161.6 0.0 copy-done.2
  161.6 0.6 convert_reduce_fusion
  162.2 38.8 %psum.29 = f32[]{:T(128)} all-reduce(f32[]{:T(128)} %get-tuple-element.3), channel_id=1, replica_groups=mesh['nodes'=32] {'nodes'}, use_global_device_ids=true, to_apply=%region_6.7 | all-reduce | flops 1 | bytes 8 | tf_op jit(solution)/shard_map/psum | solution.py:25
  201.1 12.9 %convolution_bitcast_fusion = f32[16384,128]{1,0:T(8,128)} fusion(bf16[512,16384]{1,0:T(8,128)(2,1)} %param.6, f32[128,40]{0,1:T(8,128)S(1)} %copy-done, f32[512,40]{0,1:T(8,128)S(1)} %get-tuple-element.10, f32[]{:T(128)} %psum.29, f32[512]{0:T(512)S(1)} %convert_element_type.31, f32[512]{0:T(512)S(1)} %log.9, f32[512]{0:T(512)S(1)} %get-tuple-element.9, ...), kind=kOutput, calls=%fused_computation | convolution fusion | flops 2152961024 | bytes 25276420 | tf_op jit(solution)/shard_map/dot_general | solution.py:32
  214.0 0.0 reduce-scatter.2.cloned.1.call-update
  214.0 0.0 all-reduce.3.cloned.1.call-start
  214.0 148.6 %reduce-scatter.2.cloned.1.call-done = f32[512,128]{1,0:T(8,128)} async-done(((f32[16384,128]{1,0:T(8,128)}), f32[512,128]{1,0:T(8,128)}) %reduce-scatter.2.cloned.1.call-update) | async-done | bytes 262160 | tf_op jit(solution)/shard_map/reduce_scatter | solution.py:33
  362.6 1.8 fusion
  364.4 0.0 all-reduce.3.cloned.1.call-update
  364.4 0.8 fusion.9
  365.9 37.3 %all-reduce = (f32[]{:T(128)}, f32[128,40]{0,1:T(8,128)}) all-reduce(f32[]{:T(128)S(6)} %neg.3, f32[128,40]{0,1:T(8,128)S(1)} %fusion.9), channel_id=1, replica_groups=mesh['nodes'=32] {'nodes'}, use_global_device_ids=true, to_apply=%region_4.5 | all-reduce | flops 5121 | bytes 40968 | tf_op jit(solution)/shard_map/psum | solution.py:28
  404.6 87.4 %all-reduce.3.cloned.1.call-done = f32[128,128]{1,0:T(8,128)} async-done(((f32[128,128]{1,0:T(8,128)}), f32[128,128]{1,0:T(8,128)}) %all-reduce.3.cloned.1.call-update) | async-done | bytes 65552 | tf_op jit(solution)/shard_map/psum | solution.py:35
  492.0 1.5 copy.10
  (4 shorter events, 0.1 us)
Async XLA Ops:
  7.2 80.0 %copy-start.1 = (f32[128,128]{1,0:T(8,128)S(1)}, f32[128,128]{1,0:T(8,128)}, u32[]{:S(2)}) copy-start(f32[128,128]{1,0:T(8,128)} %param.8) | copy-start | bytes 196612
  7.2 80.9 %copy-start.3 = (s32[512]{0:T(512)S(1)}, s32[512]{0:T(512)}, u32[]{:S(2)}) copy-start(s32[512]{0:T(512)} %param.11) | copy-start | bytes 6148
  7.2 68.5 %all-gather.3.cloned.1.call-start = ((), (), s32[]{:S(2)}) async-start(), calls=%async_computation.1 | async-start | bytes 4325376 | tf_op jit(solution)/shard_map/all_gather | solution.py:17
  7.9 153.5 %copy-start = (f32[128,40]{0,1:T(8,128)S(1)}, f32[128,40]{0,1:T(8,128)}, u32[]{:S(2)}) copy-start(f32[128,40]{0,1:T(8,128)} %param.9) | copy-start | bytes 61444
  7.9 153.7 %copy-start.2 = (s32[512]{0:T(512)S(1)}, s32[512]{0:T(512)}, u32[]{:S(2)}) copy-start(s32[512]{0:T(512)} %param.10) | copy-start | bytes 6148
  7.9 140.7 %all-gather.5.cloned.1.call-start = ((), (), s32[]{:S(2)}) async-start(), calls=%async_computation.2 | async-start | bytes 4325376 | tf_op jit(solution)/shard_map/all_gather | solution.py:21
  88.0 274.6 %reduce-scatter.2.cloned.1.call-start = ((), (), s32[]{:S(2)}) async-start(), calls=%async_computation.3 | async-start | bytes 8650752 | tf_op jit(solution)/shard_map/reduce_scatter | solution.py:33
  214.0 278.0 %all-reduce.3.cloned.1.call-start = ((), (), s32[]{:S(2)}) async-start(), calls=%async_computation.4 | async-start | bytes 131072 | tf_op jit(solution)/shard_map/psum | solution.py:35
Sparse Core Ops, SparseCore 0:
  10.8 64.8 all-gather.2
  88.1 60.4 all-gather.4
  214.1 148.4 reduce-scatter.1
  368.6 123.3 all-reduce.2
where the time goes:
time: 502 us; the launch traced here: 501 us
  waiting for transfers between devices  365 us (73%)
  blocking collectives  76.2 us (15%)
  matrix products  40.6 us (8%)
  between operations  17 us (3%)
    reduce_scatter x1, waiting for transfers between devices, local_step(): lax.psum_scatter(part_sums, axis_name, scatter_dimension=0, tiled=True)  149 us
    psum x1, waiting for transfers between devices, local_step(): lax.psum(lax.dot_general(agg_one, grad_one, ROW_CONTRACT, preferred_eleme...  87.4 us
    all_gather x1, waiting for transfers between devices, local_step(): feats_all = lax.all_gather(feat_rows, axis_name, tiled=True)  67.7 us
    all_gather x1, waiting for transfers between devices, local_step(): hidden_all = lax.all_gather(hidden, axis_name, tiled=True)  60.6 us
    psum x1, blocking collectives, local_step(): label_count = lax.psum(jnp.sum(weight), axis_name)  38.8 us
    psum x1, blocking collectives, local_step(): lax.psum(-jnp.sum(weight * jnp.sum(onehot * log_prob, axis=-1)), axis_name)  37.3 us
    dot_general x1, matrix products, local_step(): lax.dot_general(adj_rows, back_two, ROW_CONTRACT, preferred_element_type=...  12.9 us
    dot_general x1, matrix products, local_step(): jnp.dot(adj_rows, hidden_all, preferred_element_type=jnp.float32)  12.7 us
  transfers between devices with their start and end apart: 4, of which 4 were waited for; matrix products, arithmetic and copies ran while one was open for 0% of the time, Pallas kernels for 0%

commit v1 on v0

v1 whole, which is shorter than its diff:
```python
import functools

import jax
import jax.numpy as jnp
from jax import lax
from jax.experimental import pallas as pl
from jax.experimental.pallas import tpu as pltpu
from jax.sharding import PartitionSpec as P

MESH = pl.DeviceIdType.MESH
F32 = jnp.float32
BF16 = jnp.bfloat16
NDEV = 32
HALVES = 2
F = 128
K = 40
KP = 48
TAIL = 16

STEPS = [[(q, t - (q + 1) // 2) for q in range(4) if 0 <= t - (q + 1) // 2 < 4] for t in range(6)]


def kernel(axis, rows, a_hbm, x_hbm, w1_ref, w2_ref, lab_ref, mask_ref, loss_out, dw1_out, dw2_out,
           a_v, xall, hall, acc, s1, s1t, z1t, w2p, ut, mrow, sq,
           own, outbox, pairin, xin, yin, zin, sums,
           ar1_src, ar1_pin, ar1_pl, ar1_zz, ar1_fin, ar2_src, ar2_pin, ar2_pl, ar2_zz, ar2_fin,
           a_sem, x_sem, ag1_r, ag1_s, ag2_r, ag2_s, rs_ps, rs_pr, rs_xs, rs_xr, rs_ys, rs_yr, rs_zs, rs_zr,
           ar1_s, ar1_r, ar2_s, ar2_r):
    me = lax.axis_index(axis)
    core = me % 2
    x = (me // 2) % 2
    y = (me // 4) % 2
    z = me // 8
    mid = ((z + 1) // 2) % 2
    half = z // 2
    z_in = 1 + z % 2
    z_out = (3 * z - 3) * mid + z * (1 - mid)

    def dev(xx, yy, zz, cc):
        return ((zz * 2 + yy) * 2 + xx) * 2 + cc

    xn, yn = dev(1 - x, y, z, core), dev(x, 1 - y, z, core)
    dn, pn = dev(1 - x, 1 - y, z, core), dev(x, y, z, 1 - core)
    zin_n, zout_n = dev(x, y, z_in, core), dev(x, y, z_out, core)
    zothers = [dev(x, y, (z + k) % 4, core) for k in (1, 2, 3)]

    def zk(j):
        late = j // 2
        line = late * j + (1 - late) * (j + mid * (1 - 2 * j))
        return line + half * (3 - 2 * line)

    def bid(q, j, other=0):
        qx, qy = q % 2, q // 2
        cc = core + other * (1 - 2 * core)
        return dev(x + qx * (1 - 2 * x), y + qy * (1 - 2 * y), zk(j), cc)

    def rcopy(src, dst, ssem, rsem, to):
        return pltpu.make_async_remote_copy(src_ref=src, dst_ref=dst, send_sem=ssem, recv_sem=rsem, device_id=(to,),
                                            device_id_type=MESH)

    def a_copy(b):
        cols = pl.ds(pl.multiple_of(b * rows, rows), rows)
        return pltpu.make_async_copy(a_hbm.at[:, cols], a_v.at[b], a_sem.at[b])

    x_copy = pltpu.make_async_copy(x_hbm, xall.at[me, pl.ds(0, rows)], x_sem)
    x_copy.start()
    for t in range(6):
        for q, j in STEPS[t]:
            a_copy(bid(q, j)).start()
            a_copy(bid(q, j, 1)).start()
    barrier = pltpu.get_barrier_semaphore()
    for to in [pn, xn, yn, dn] + zothers:
        pl.semaphore_signal(barrier, inc=1, device_id=(to,), device_id_type=MESH)
    mrow[...] = jnp.zeros_like(mrow)
    mrow[0:rows // 128, :] = mask_ref[...].astype(F32)
    xall[me, rows:rows + TAIL, :] = mrow[...].astype(BF16)
    w2p[...] = jnp.zeros_like(w2p)
    w2p[:, 0:K] = w2_ref[...]
    w1b = w1_ref[...].astype(BF16)
    acc[...] = jnp.zeros_like(acc)
    x_copy.wait()
    pl.semaphore_wait(barrier, 7)

    def gather(buf, cuts, r_sem, s_sem, first):
        pending = []

        def chunk(b, h):
            return buf.at[b, pl.ds(cuts[h], cuts[h + 1] - cuts[h])]

        def send(b, h, to, cond=None):
            k = len(pending)
            c = rcopy(chunk(b, h), chunk(b, h), s_sem.at[k], r_sem.at[b, h], to)
            pending.append((c, cond))
            if cond is None:
                c.start()
            else:
                pl.when(cond)(c.start)

        def wait_recv(b, h):
            rcopy(chunk(b, h), chunk(b, h), s_sem.at[0], r_sem.at[b, h], pn).wait_recv()

        def mul(b):
            if first:
                a_copy(b).wait()
            acc[...] += jnp.dot(a_v[b], buf[b, 0:rows, :], preferred_element_type=F32)

        is_mid = mid == 1

        def forward(q, j, h):
            b = bid(q, j)
            if q == 0:
                if j == 0:
                    send(b, h, zin_n)
                    send(b, h, zout_n, is_mid)
                elif j == 1:
                    send(b, h, zin_n, is_mid)
                else:
                    send(b, h, zout_n, is_mid)
                send(b, h, xn)
                send(b, h, yn)
            elif q == 1 and j % 2 == 1:
                send(b, h, yn)
            elif q == 2 and j % 2 == 0:
                send(b, h, xn)
            send(b, h, pn)

        def mul_loop(t, other):
            qs = [q for q, _ in STEPS[t]]

            def body(q, carry):
                b = bid(q, t - (q + 1) // 2, other)
                if other:
                    for h in range(HALVES):
                        wait_recv(b, h)
                mul(b)
                return carry
            lax.fori_loop(qs[0], qs[-1] + 1, body, 0)

        for t in range(7):
            if t < 6:
                for h in range(HALVES):
                    for q, j in STEPS[t]:
                        if t > 0:
                            wait_recv(bid(q, j), h)
                        forward(q, j, h)
                mul_loop(t, 0)
            if t > 0:
                mul_loop(t - 1, 1)
        return pending

    def drain(pending):
        for c, cond in pending:
            if cond is None:
                c.wait_send()
            else:
                pl.when(cond)(c.wait_send)

    hr = rows // HALVES
    cuts1 = [h * hr for h in range(HALVES)] + [rows + TAIL]
    cuts2 = [h * hr for h in range(HALVES)] + [rows]
    sends1 = gather(xall, cuts1, ag1_r, ag1_s, True)

    s1b = acc[...].astype(BF16)
    s1[...] = s1b
    z1 = jnp.dot(s1b, w1b, preferred_element_type=F32)
    hall[me] = jnp.maximum(z1, 0.0).astype(BF16)
    sq[...] = z1
    acc[...] = jnp.zeros_like(acc)

    sends2 = gather(hall, cuts2, ag2_r, ag2_s, False)

    w2b = w2p[...].astype(BF16)
    w2t = w2p[...].T[0:KP, :].astype(BF16)

    def count_body(b, tot):
        return tot + xall[b, rows:rows + TAIL, :].astype(F32)
    label_count = jnp.sum(lax.fori_loop(0, NDEV, count_body, jnp.zeros((TAIL, 128), F32)))
    s2b = acc[...].astype(BF16)
    z2 = lax.dot_general(w2t, s2b, (((1,), (1,)), ((), ())), preferred_element_type=F32)
    row_id = lax.broadcasted_iota(jnp.int32, (KP, rows), 0)
    valid = row_id < K
    top = jnp.max(jnp.where(valid, z2, -jnp.inf), axis=0, keepdims=True)
    shifted = jnp.where(valid, z2 - top, 0.0)
    norm = jnp.log(jnp.sum(jnp.where(valid, jnp.exp(shifted), 0.0), axis=0, keepdims=True))
    log_prob = shifted - norm
    hot = row_id == lab_ref[...]
    onehot = jnp.where(hot, 1.0, 0.0)
    weight = jnp.concatenate([mrow[k:k + 1, :] for k in range(rows // 128)], axis=1)
    loss_row = -weight * jnp.sum(jnp.where(hot, log_prob, 0.0), axis=0, keepdims=True)
    g2 = jnp.where(valid, weight * (jnp.exp(log_prob) - onehot) / label_count, 0.0).astype(BF16)
    ut[...] = jnp.dot(w2b[:, 0:KP], g2, preferred_element_type=F32).astype(BF16)
    dw2t = jnp.dot(g2, s2b, preferred_element_type=F32)
    loss_part = loss_row[:, 0:128]
    for k in range(1, rows // 128):
        loss_part = loss_part + loss_row[:, k * 128:(k + 1) * 128]
    ar2_src[...] = dw2t
    ar2_src[K:K + 1, :] = loss_part

    plane = y * 2 + x

    def make_ar(src, pin, pl4, zz, fin, s_sem, r_sem):
        n = src.shape[0] // 2
        sends = []

        def go(c):
            c.start()
            sends.append(c)

        def s1():
            lo = pl.multiple_of((1 - core) * n, n)
            go(rcopy(src.at[pl.ds(lo, n)], pin, s_sem.at[0], r_sem.at[0], pn))

        def s2():
            rcopy(pin, pin, s_sem.at[0], r_sem.at[0], pn).wait_recv()
            lo = pl.multiple_of(core * n, n)
            pl4[plane] = src[pl.ds(lo, n), :] + pin[...]
            for k, to in enumerate((xn, yn, dn)):
                go(rcopy(pl4.at[plane], pl4.at[plane], s_sem.at[1 + k], r_sem.at[1 + plane], to))

        def s3():
            for px, py in ((1, 0), (0, 1), (1, 1)):
                p = (y + py * (1 - 2 * y)) * 2 + x + px * (1 - 2 * x)
                rcopy(pl4.at[p], pl4.at[p], s_sem.at[0], r_sem.at[1 + p], pn).wait_recv()
            zz[z] = (pl4[0] + pl4[1]) + (pl4[2] + pl4[3])
            for k, to in enumerate(zothers):
                go(rcopy(zz.at[z], zz.at[z], s_sem.at[4 + k], r_sem.at[5 + z], to))

        def s4():
            for k in (1, 2, 3):
                o = (z + k) % 4
                rcopy(zz.at[o], zz.at[o], s_sem.at[0], r_sem.at[5 + o], pn).wait_recv()
            fin[core] = (zz[0] + zz[1]) + (zz[2] + zz[3])
            go(rcopy(fin.at[core], fin.at[core], s_sem.at[7], r_sem.at[9], pn))

        def s5():
            rcopy(fin.at[1 - core], fin.at[1 - core], s_sem.at[0], r_sem.at[9], pn).wait_recv()
            for c in sends:
                c.wait_send()

        return s1, s2, s3, s4, s5

    small = make_ar(ar2_src, ar2_pin, ar2_pl, ar2_zz, ar2_fin, ar2_s, ar2_r)
    small[0]()

    def parts(q, j):
        i = q * 4 + j
        outbox[i] = jnp.dot(ut[...], a_v[bid(q, j, 1)], preferred_element_type=F32)
        rcopy(outbox.at[i], pairin.at[i], rs_ps.at[i], rs_pr.at[i], pn).start()
        own[i] = jnp.dot(ut[...], a_v[bid(q, j)], preferred_element_type=F32)

    def diag_body(k, carry):
        parts(3, 3 - k)
        return carry

    def side_body(k, carry):
        parts(1 + k % 2, 3 - k // 2)
        return carry

    def own_body(k, carry):
        parts(0, 3 - k)
        return carry

    fh = F // HALVES

    def hs(h):
        return pl.ds(h * fh, fh)

    def pair_add(q, j):
        i = q * 4 + j
        rcopy(pairin.at[i], pairin.at[i], rs_ps.at[0], rs_pr.at[i], pn).wait_recv()
        own[i] = own[i] + pairin[i]

    def xslot(q, j):
        return 2 + j if q == 0 else (3 - j) // 2

    rs_sends = []

    def rs_send(src, dst, s_arr, r_arr, k, h, dk, to):
        c = rcopy(src, dst, s_arr.at[k, h], r_arr.at[dk, h], to)
        c.start()
        rs_sends.append(c)

    lax.fori_loop(0, 4, diag_body, 0)
    for j in (3, 2, 1, 0):
        pair_add(3, j)
        for h in range(HALVES):
            if j % 2 == 1:
                s = xslot(2, j)
                rs_send(own.at[12 + j, hs(h)], xin.at[s, hs(h)], rs_xs, rs_xr, s, h, s, xn)
            else:
                s = xslot(1, j)
                rs_send(own.at[12 + j, hs(h)], yin.at[s, hs(h)], rs_ys, rs_yr, s, h, s, yn)
    lax.fori_loop(0, 8, side_body, 0)
    small[1]()
    lax.fori_loop(0, 4, own_body, 0)
    for j in (3, 2, 1, 0):
        pair_add(1, j)
        pair_add(2, j)
    for j in (3, 2, 1, 0):
        for h in range(HALVES):
            ix, iy = 4 + j, 8 + j
            if j % 2 == 1:
                s = xslot(2, j)
                rcopy(xin.at[s, hs(h)], xin.at[s, hs(h)], rs_xs.at[0, 0], rs_xr.at[s, h], pn).wait_recv()
                own[iy, hs(h)] = own[iy, hs(h)] + xin[s, hs(h)]
            else:
                s = xslot(1, j)
                rcopy(yin.at[s, hs(h)], yin.at[s, hs(h)], rs_ys.at[0, 0], rs_yr.at[s, h], pn).wait_recv()
                own[ix, hs(h)] = own[ix, hs(h)] + yin[s, hs(h)]
            rs_send(own.at[ix, hs(h)], xin.at[2 + j, hs(h)], rs_xs, rs_xr, 2 + j, h, 2 + j, xn)
            rs_send(own.at[iy, hs(h)], yin.at[2 + j, hs(h)], rs_ys, rs_yr, 2 + j, h, 2 + j, yn)
    for j in (3, 2, 1, 0):
        pair_add(0, j)
    small[2]()

    z1t[...] = sq[...].T
    s1t[...] = s1[...].astype(F32).T.astype(BF16)

    def z_wait(s, h):
        rcopy(zin.at[s, hs(h)], zin.at[s, hs(h)], rs_zs.at[0, 0], rs_zr.at[s, h], pn).wait_recv()

    for j in (3, 2, 1, 0):
        for h in range(HALVES):
            for arr, r_arr in ((xin, rs_xr), (yin, rs_yr)):
                rcopy(arr.at[2 + j, hs(h)], arr.at[2 + j, hs(h)], rs_xs.at[0, 0], r_arr.at[2 + j, h], pn).wait_recv()
            sums[j, hs(h)] = (own[j, hs(h)] + xin[2 + j, hs(h)]) + yin[2 + j, hs(h)]

            @pl.when(mid == 1)
            def _():
                s = {3: 3, 2: 2, 1: 5, 0: 0}[j]
                z_wait(s, h)
                sums[j, hs(h)] = sums[j, hs(h)] + zin[s, hs(h)]
            if j > 0:
                to = zin_n if j > 1 else dev(x, y, z_in + mid * (z_out - z_in), core)
                slot = j + 2 * mid if j > 1 else 4 * mid
                rs_send(sums.at[j, hs(h)], zin.at[slot, hs(h)], rs_zs, rs_zr, j, h, slot, to)
            else:
                z_wait(4, h)
                sums[0, hs(h)] = sums[0, hs(h)] + zin[4, hs(h)]
        if j == 3:
            small[3]()

    g1t = jnp.where(z1t[...] > 0.0, sums[0], 0.0).astype(BF16)
    ar1_src[...] = lax.dot_general(s1t[...], g1t, (((1,), (1,)), ((), ())), preferred_element_type=F32)
    big = make_ar(ar1_src, ar1_pin, ar1_pl, ar1_zz, ar1_fin, ar1_s, ar1_r)
    big[0]()
    small[4]()
    w2p[0:KP // 2, :] = ar2_fin[0]
    w2p[KP // 2:KP, :] = ar2_fin[1]
    loss_out[0] = jnp.sum(w2p[K:K + 1, :]) / label_count
    dw2_out[...] = w2p[...].T[:, 0:K]
    big[1]()
    drain(sends1)
    drain(sends2)
    big[2]()
    for c in rs_sends:
        c.wait_send()
    for i in range(16):
        rcopy(outbox.at[i], pairin.at[i], rs_ps.at[i], rs_pr.at[i], pn).wait_send()
    big[3]()
    big[4]()
    dw1_out[0:F // 2, :] = ar1_fin[0]
    dw1_out[F // 2:F, :] = ar1_fin[1]


def solution(mesh):
    axis = 'nodes'

    def local_step(adj_rows, feat_rows, w_one, w_two, label_rows, mask_rows):
        rows = adj_rows.shape[0]
        dma = pltpu.SemaphoreType.DMA
        nsend = 64 * HALVES
        blk = lambda n: pltpu.VMEM((n, F, rows), F32)
        ar = lambda n: [pltpu.VMEM((2 * n, F), F32), pltpu.VMEM((n, F), F32), pltpu.VMEM((4, n, F), F32),
                        pltpu.VMEM((4, n, F), F32), pltpu.VMEM((2, n, F), F32)]
        vmem = pl.BlockSpec(memory_space=pltpu.VMEM)
        hbm = pl.BlockSpec(memory_space=pl.ANY)
        return pl.pallas_call(
            functools.partial(kernel, axis, rows),
            name='gcn_step',
            out_shape=(jax.ShapeDtypeStruct((1,), F32), jax.ShapeDtypeStruct((F, F), F32),
                       jax.ShapeDtypeStruct((F, K), F32)),
            in_specs=[hbm, hbm, vmem, vmem, vmem, vmem],
            out_specs=(pl.BlockSpec(memory_space=pltpu.SMEM), vmem, vmem),
            scratch_shapes=[
                pltpu.VMEM((NDEV, rows, rows), BF16), pltpu.VMEM((NDEV, rows + TAIL, F), BF16),
                pltpu.VMEM((NDEV, rows, F), BF16), pltpu.VMEM((rows, F), F32), pltpu.VMEM((rows, F), BF16),
                pltpu.VMEM((F, rows), BF16), pltpu.VMEM((F, rows), F32), pltpu.VMEM((F, F), F32),
                pltpu.VMEM((F, rows), BF16), pltpu.VMEM((TAIL, F), F32), pltpu.VMEM((rows, F), F32),
                blk(16), blk(16), blk(16), blk(6), blk(6), blk(6), blk(4),
                *ar(F // 2), *ar(KP // 2),
                dma((NDEV,)), dma(()), dma((NDEV, HALVES)), dma((nsend,)), dma((NDEV, HALVES)), dma((nsend,)),
                dma((16,)), dma((16,)), dma((6, HALVES)), dma((6, HALVES)), dma((6, HALVES)), dma((6, HALVES)),
                dma((6, HALVES)), dma((6, HALVES)), dma((8,)), dma((10,)), dma((8,)), dma((10,)),
            ],
            compiler_params=pltpu.CompilerParams(collective_id=0, has_side_effects=True,
                                                 vmem_limit_bytes=60 * 1024 * 1024),
        )(adj_rows, feat_rows, w_one, w_two, label_rows.reshape(1, rows), mask_rows.reshape(rows // 128, 128))

    return jax.shard_map(local_step, mesh=mesh,
                         in_specs=(P(axis, None), P(axis, None), P(None, None), P(None, None), P(axis), P(axis)),
                         out_specs=(P(None), P(None, None), P(None, None)), check_vma=False)
```

time: 502 us -> 126 us (0.25)
  waiting for transfers between devices: 365 us -> 0 us
  Pallas kernels: 0 us -> 119 us
  blocking collectives: 76.2 us -> 0 us
  matrix products: 40.6 us -> 0 us
  between operations: 17 us -> 2.45 us
    reduce_scatter x1 -> x0, waiting for transfers between devices: 149 us -> none  [local_step(): lax.psum_scatter(part_sums, axis_name, scatter_dimension=0, tiled=True)]
    all_gather x2 -> x0, waiting for transfers between devices: 128 us -> none  [the longest x1 67.7 us: local_step(): feats_all = lax.all_gather(feat_rows, axis_name, tiled=True)]
    pallas_call x0 -> x1, Pallas kernels: none -> 119 us  [local_step(): pl.pallas_call(functools.partial(kernel, axis, rows), name='gcn_step', ou...]
    psum x1 -> x0, waiting for transfers between devices: 87.4 us -> none  [local_step(): lax.psum(lax.dot_general(agg_one, grad_one, ROW_CONTRACT, preferred_eleme...]
    psum x2 -> x0, blocking collectives: 76.2 us -> none  [the longest x1 38.8 us: local_step(): label_count = lax.psum(jnp.sum(weight), axis_name)]
    dot_general x7 -> x0, matrix products: 40.6 us -> none  [the longest x1 12.9 us: local_step(): lax.dot_general(adj_rows, back_two, ROW_CONTRACT, preferred_element_type=...]
  transfers between devices with their start and end apart: 4 -> 0, of which waited for: 4 -> 0; matrix products, arithmetic and copies ran while one was open for 0% -> 0% of each run, Pallas kernels for 0% -> 0%
where the time goes in v1:
time: 126 us
  Pallas kernels  119 us (94%)
  local copies, waits for them, and re-layouts  4.45 us (4%)
  between operations  2.45 us (2%)
    pallas_call x1, Pallas kernels, local_step(): pl.pallas_call(functools.partial(kernel, axis, rows), name='gcn_step', ou...  119 us
    unnamed x2, local copies, waits for them, and re-layouts  2.93 us

profile of v1, /device:TPU:0, one launch (start us, length us, event | category | flops | bytes accessed | tf_op | source)
XLA Modules:
  0.0 125.7 jit_solution(4307999797020908458)
XLA Ops:
  0.6 1.5 %copy.9.w2_ref = f32[128,40]{1,0:T(8,128)} copy(f32[128,40]{0,1:T(8,128)} %param.9) | data formatting | bytes 40960 | tf_op args[3]
  2.1 118.8 %gcn_step.1 = (f32[1]{0:T(128)}, f32[128,128]{1,0:T(8,128)}, f32[128,40]{1,0:T(8,128)}) custom-call(bf16[512,16384]{1,0:T(8,128)(2,1)} %a_hbm.1, bf16[512,128]{1,0:T(8,128)(2,1)} %x_hbm.1, f32[128,128]{1,0:T(8,128)} %w1_ref.1, f32[128,40]{1,0:T(8,128)} %copy.9.w2_ref, s32[1,512]{1,0:T(1,128)} %bitcast.2, s32[4,128]{1,0:T(4,128)} %bitcast.3), custom_call_target="tpu_custom_call" | custom-call | tf_op jit(solution)/shard_map/gcn_step/pallas_call | solution.py:378
  120.9 1.5 %copy.10 = f32[128,40]{0,1:T(8,128)} copy(f32[128,40]{1,0:T(8,128)} %get-tuple-element.5) | data formatting | bytes 40960 | tf_op jit(solution)/shard_map/gcn_step/pallas_call | solution.py:378
  123.1 1.5 %copy.14 = f32[128,128]{1,0:T(8,128)} copy(f32[128,128]{1,0:T(8,128)} %get-tuple-element.10) | data formatting | bytes 131072

commit v2 on v1

--- a/solution.py
+++ b/solution.py
@@ -17,10 +17,34 @@
 KP = 48
 TAIL = 16
 
-STEPS = [[(q, t - (q + 1) // 2) for q in range(4) if 0 <= t - (q + 1) // 2 < 4] for t in range(6)]
-
-
-def kernel(axis, rows, a_hbm, x_hbm, w1_ref, w2_ref, lab_ref, mask_ref, loss_out, dw1_out, dw2_out,
+ORDER_END = (
+    0, 16, 32, 1, 17, 40, 8, 2, 36, 5, 18, 21, 33, 44, 37, 24, 3, 12, 19, 34, 38, 10, 22, 28,
+    29, 13, 26, 4, 7, 9, 6, 45, 23, 43, 41, 42, 11, 20, 39, 27, 25, 15, 30, 14, 46, 35, 47, 31,
+)
+ORDER_MID = (
+    0, 16, 32, 2, 1, 18, 17, 36, 40, 3, 19, 10, 41, 26, 24, 34, 5, 38, 37, 42, 21, 44, 33, 4,
+    43, 11, 20, 7, 45, 39, 8, 23, 9, 46, 27, 35, 22, 47, 14, 25, 30, 6, 15, 31, 13, 28, 29, 12,
+)
+PIECES = 3
+BATCH = 4
+
+
+def program(order):
+    seen, steps, ready, late, following = {}, [], [], [], []
+    for code in order:
+        c, q, j = code // 16, code // 4 % 4, code % 4
+        steps.append((c, q, j))
+        seen[q, j] = seen.get((q, j), 0) + 1
+        if seen[q, j] == PIECES:
+            ready.append((q, j))
+            following.append((q, j))
+            if len(ready) + len(late) >= BATCH:
+                steps.append((ready, late))
+                ready, late, following = [], following, []
+    return steps + [(ready, late), ([], following)]
+
+
+def kernel(axis, rows, a_hbm, x_hbm, w1_ref, w2_ref, lab_ref, mask_ref, out_ref,
            a_v, xall, hall, acc, s1, s1t, z1t, w2p, ut, mrow, sq,
            own, outbox, pairin, xin, yin, zin, sums,
            ar1_src, ar1_pin, ar1_pl, ar1_zz, ar1_fin, ar2_src, ar2_pin, ar2_pl, ar2_zz, ar2_fin,
@@ -64,10 +88,9 @@
 
     x_copy = pltpu.make_async_copy(x_hbm, xall.at[me, pl.ds(0, rows)], x_sem)
     x_copy.start()
-    for t in range(6):
-        for q, j in STEPS[t]:
-            a_copy(bid(q, j)).start()
-            a_copy(bid(q, j, 1)).start()
+    blocks = {(q, j, o): bid(q, j, o) for q in range(4) for j in range(4) for o in range(2)}
+    for b in blocks.values():
+        a_copy(b).start()
     barrier = pltpu.get_barrier_semaphore()
     for to in [pn, xn, yn, dn] + zothers:
         pl.semaphore_signal(barrier, inc=1, device_id=(to,), device_id_type=MESH)
@@ -75,90 +98,95 @@
     mrow[0:rows // 128, :] = mask_ref[...].astype(F32)
     xall[me, rows:rows + TAIL, :] = mrow[...].astype(BF16)
     w2p[...] = jnp.zeros_like(w2p)
-    w2p[:, 0:K] = w2_ref[...]
+    w2p[0:K, :] = w2_ref[...]
     w1b = w1_ref[...].astype(BF16)
     acc[...] = jnp.zeros_like(acc)
     x_copy.wait()
     pl.semaphore_wait(barrier, 7)
 
+    is_mid = mid == 1
+
+    def pick(i, values):
+        out = values[0]
+        for k in range(1, len(values)):
+            out = jnp.where(i == k, values[k], out)
+        return out
+
     def gather(buf, cuts, r_sem, s_sem, first):
-        pending = []
-
-        def chunk(b, h):
-            return buf.at[b, pl.ds(cuts[h], cuts[h + 1] - cuts[h])]
-
-        def send(b, h, to, cond=None):
-            k = len(pending)
-            c = rcopy(chunk(b, h), chunk(b, h), s_sem.at[k], r_sem.at[b, h], to)
-            pending.append((c, cond))
-            if cond is None:
-                c.start()
-            else:
-                pl.when(cond)(c.start)
-
-        def wait_recv(b, h):
-            rcopy(chunk(b, h), chunk(b, h), s_sem.at[0], r_sem.at[b, h], pn).wait_recv()
-
-        def mul(b):
-            if first:
-                a_copy(b).wait()
-            acc[...] += jnp.dot(a_v[b], buf[b, 0:rows, :], preferred_element_type=F32)
-
-        is_mid = mid == 1
-
-        def forward(q, j, h):
-            b = bid(q, j)
-            if q == 0:
+        def piece(b, c):
+            return buf.at[b, pl.ds(cuts[c], cuts[c + 1] - cuts[c])]
+
+        def wait_recv(b, c):
+            rcopy(piece(b, c), piece(b, c), s_sem.at[0], r_sem.at[b, c], pn).wait_recv()
+
+        def targets(c, q, j, between):
+            to = []
+            if q == 0 or c == 2:
                 if j == 0:
-                    send(b, h, zin_n)
-                    send(b, h, zout_n, is_mid)
-                elif j == 1:
-                    send(b, h, zin_n, is_mid)
-                else:
-                    send(b, h, zout_n, is_mid)
-                send(b, h, xn)
-                send(b, h, yn)
-            elif q == 1 and j % 2 == 1:
-                send(b, h, yn)
-            elif q == 2 and j % 2 == 0:
-                send(b, h, xn)
-            send(b, h, pn)
-
-        def mul_loop(t, other):
-            qs = [q for q, _ in STEPS[t]]
-
-            def body(q, carry):
-                b = bid(q, t - (q + 1) // 2, other)
-                if other:
-                    for h in range(HALVES):
-                        wait_recv(b, h)
-                mul(b)
+                    to += [zin_n, zout_n] if between else [zin_n]
+                elif between:
+                    to += [zin_n if j == 1 else zout_n]
+            if q == 0 and (c < 2 or j == 0):
+                to += [xn, yn]
+            elif (q == 2 and c < 2 and j % 2 == 0) or (q == 2 and c == 2 and j == 0):
+                to += [xn]
+            elif q == 1 and c < 2 and j % 2 == 1:
+                to += [yn]
+            return to + [pn]
+
+        def multiply(ready, late):
+            ids = [blocks[q, j, 0] for q, j in ready] + [blocks[q, j, 1] for q, j in late]
+            if not ids:
+                return
+
+            def body(i, carry):
+                b = pick(i, ids)
+                if late:
+                    @pl.when(i >= len(ready))
+                    def _():
+                        for c in range(PIECES):
+                            wait_recv(b, c)
+                if first:
+                    a_copy(b).wait()
+                acc[...] += jnp.dot(a_v[b], buf[b, 0:rows, :], preferred_element_type=F32)
                 return carry
-            lax.fori_loop(qs[0], qs[-1] + 1, body, 0)
-
-        for t in range(7):
-            if t < 6:
-                for h in range(HALVES):
-                    for q, j in STEPS[t]:
-                        if t > 0:
-                            wait_recv(bid(q, j), h)
-                        forward(q, j, h)
-                mul_loop(t, 0)
-            if t > 0:
-                mul_loop(t - 1, 1)
-        return pending
-
-    def drain(pending):
-        for c, cond in pending:
-            if cond is None:
-                c.wait_send()
-            else:
-                pl.when(cond)(c.wait_send)
-
-    hr = rows // HALVES
-    cuts1 = [h * hr for h in range(HALVES)] + [rows + TAIL]
-    cuts2 = [h * hr for h in range(HALVES)] + [rows]
-    sends1 = gather(xall, cuts1, ag1_r, ag1_s, True)
+            lax.fori_loop(0, len(ids), body, 0)
+
+        def run(order, between, pending):
+            for step in program(order):
+                if len(step) == 2:
+                    multiply(*step)
+                    continue
+                c, q, j = step
+                b = blocks[q, j, 0]
+                if (q, j) != (0, 0):
+                    wait_recv(b, c)
+                for to in targets(c, q, j, between):
+                    k = len(pending)
+                    rcopy(piece(b, c), piece(b, c), s_sem.at[k], r_sem.at[b, c], to).start()
+                    pending.append((b, c, to))
+
+        sent = {True: [], False: []}
+
+        @pl.when(is_mid)
+        def _():
+            run(ORDER_MID, True, sent[True])
+
+        @pl.when(mid == 0)
+        def _():
+            run(ORDER_END, False, sent[False])
+
+        def drain():
+            for between, when in ((True, is_mid), (False, mid == 0)):
+                @pl.when(when)
+                def _():
+                    for k, (b, c, to) in enumerate(sent[between]):
+                        rcopy(piece(b, c), piece(b, c), s_sem.at[k], r_sem.at[b, c], to).wait_send()
+        return drain
+
+    cuts1 = (0, rows * 3 // 8, rows * 6 // 8, rows + TAIL)
+    cuts2 = (0, rows * 3 // 8, rows * 6 // 8, rows)
+    drain1 = gather(xall, cuts1, ag1_r, ag1_s, True)
 
     s1b = acc[...].astype(BF16)
     s1[...] = s1b
@@ -167,10 +195,10 @@
     sq[...] = z1
     acc[...] = jnp.zeros_like(acc)
 
-    sends2 = gather(hall, cuts2, ag2_r, ag2_s, False)
-
-    w2b = w2p[...].astype(BF16)
-    w2t = w2p[...].T[0:KP, :].astype(BF16)
+    drain2 = gather(hall, cuts2, ag2_r, ag2_s, False)
+
+    w2b = w2p[...].T.astype(BF16)
+    w2t = w2p[0:KP, :].astype(BF16)
 
     def count_body(b, tot):
         return tot + xall[b, rows:rows + TAIL, :].astype(F32)
@@ -345,13 +373,13 @@
     big = make_ar(ar1_src, ar1_pin, ar1_pl, ar1_zz, ar1_fin, ar1_s, ar1_r)
     big[0]()
     small[4]()
-    w2p[0:KP // 2, :] = ar2_fin[0]
-    w2p[KP // 2:KP, :] = ar2_fin[1]
-    loss_out[0] = jnp.sum(w2p[K:K + 1, :]) / label_count
-    dw2_out[...] = w2p[...].T[:, 0:K]
+    out_ref[F:F + KP // 2, :] = ar2_fin[0]
+    out_ref[F + KP // 2:F + KP, :] = ar2_fin[1]
+    loss_row = out_ref[F + K:F + K + 1, :]
+    out_ref[F + K:F + K + 1, :] = jnp.sum(loss_row, axis=1, keepdims=True) / label_count + jnp.zeros_like(loss_row)
     big[1]()
-    drain(sends1)
-    drain(sends2)
+    drain1()
+    drain2()
     big[2]()
     for c in rs_sends:
         c.wait_send()
@@ -359,8 +387,14 @@
         rcopy(outbox.at[i], pairin.at[i], rs_ps.at[i], rs_pr.at[i], pn).wait_send()
     big[3]()
     big[4]()
-    dw1_out[0:F // 2, :] = ar1_fin[0]
-    dw1_out[F // 2:F, :] = ar1_fin[1]
+    out_ref[0:F // 2, :] = ar1_fin[0]
+    out_ref[F // 2:F, :] = ar1_fin[1]
+
+
+def unpack(packed, loss_out, dw1_out, dw2_out):
+    loss_out[0] = packed[F + K, 0]
+    dw1_out[...] = packed[0:F, :]
+    dw2_out[...] = packed[F:F + K, :]
 
 
 def solution(mesh):
@@ -369,19 +403,18 @@
     def local_step(adj_rows, feat_rows, w_one, w_two, label_rows, mask_rows):
         rows = adj_rows.shape[0]
         dma = pltpu.SemaphoreType.DMA
-        nsend = 64 * HALVES
+        nsend = 144
         blk = lambda n: pltpu.VMEM((n, F, rows), F32)
         ar = lambda n: [pltpu.VMEM((2 * n, F), F32), pltpu.VMEM((n, F), F32), pltpu.VMEM((4, n, F), F32),
                         pltpu.VMEM((4, n, F), F32), pltpu.VMEM((2, n, F), F32)]
         vmem = pl.BlockSpec(memory_space=pltpu.VMEM)
         hbm = pl.BlockSpec(memory_space=pl.ANY)
-        return pl.pallas_call(
+        packed = pl.pallas_call(
             functools.partial(kernel, axis, rows),
             name='gcn_step',
-            out_shape=(jax.ShapeDtypeStruct((1,), F32), jax.ShapeDtypeStruct((F, F), F32),
-                       jax.ShapeDtypeStruct((F, K), F32)),
+            out_shape=jax.ShapeDtypeStruct((F + KP, F), F32),
             in_specs=[hbm, hbm, vmem, vmem, vmem, vmem],
-            out_specs=(pl.BlockSpec(memory_space=pltpu.SMEM), vmem, vmem),
+            out_specs=vmem,
             scratch_shapes=[
                 pltpu.VMEM((NDEV, rows, rows), BF16), pltpu.VMEM((NDEV, rows + TAIL, F), BF16),
                 pltpu.VMEM((NDEV, rows, F), BF16), pltpu.VMEM((rows, F), F32), pltpu.VMEM((rows, F), BF16),
@@ -389,13 +422,22 @@
                 pltpu.VMEM((F, rows), BF16), pltpu.VMEM((TAIL, F), F32), pltpu.VMEM((rows, F), F32),
                 blk(16), blk(16), blk(16), blk(6), blk(6), blk(6), blk(4),
                 *ar(F // 2), *ar(KP // 2),
-                dma((NDEV,)), dma(()), dma((NDEV, HALVES)), dma((nsend,)), dma((NDEV, HALVES)), dma((nsend,)),
+                dma((NDEV,)), dma(()), dma((NDEV, PIECES)), dma((nsend,)), dma((NDEV, PIECES)), dma((nsend,)),
                 dma((16,)), dma((16,)), dma((6, HALVES)), dma((6, HALVES)), dma((6, HALVES)), dma((6, HALVES)),
                 dma((6, HALVES)), dma((6, HALVES)), dma((8,)), dma((10,)), dma((8,)), dma((10,)),
             ],
             compiler_params=pltpu.CompilerParams(collective_id=0, has_side_effects=True,
                                                  vmem_limit_bytes=60 * 1024 * 1024),
-        )(adj_rows, feat_rows, w_one, w_two, label_rows.reshape(1, rows), mask_rows.reshape(rows // 128, 128))
+        )(adj_rows, feat_rows, w_one, w_two.T, label_rows.reshape(1, rows), mask_rows.reshape(rows // 128, 128))
+        loss, dw_one, dw_two_t = pl.pallas_call(
+            unpack,
+            name='unpack',
+            out_shape=(jax.ShapeDtypeStruct((1,), F32), jax.ShapeDtypeStruct((F, F), F32),
+                       jax.ShapeDtypeStruct((K, F), F32)),
+            in_specs=[vmem],
+            out_specs=(pl.BlockSpec(memory_space=pltpu.SMEM), vmem, vmem),
+        )(packed)
+        return loss, dw_one, dw_two_t.T
 
     return jax.shard_map(local_step, mesh=mesh,
                          in_specs=(P(axis, None), P(axis, None), P(None, None), P(None, None), P(axis), P(axis)),

time: 126 us -> 111 us (0.88)
  Pallas kernels: 119 us -> 110 us
  local copies, waits for them, and re-layouts: 4.45 us -> 0 us
  between operations: 2.45 us -> 0.64 us
    pallas_call x1, Pallas kernels: 119 us -> 109 us  [local_step(): pl.pallas_call(functools.partial(kernel, axis, rows), name='gcn_step', ou...]
    unnamed x2 -> x0, local copies, waits for them, and re-layouts: 2.93 us -> none
    pallas_call x0 -> x1, Pallas kernels: none -> 1.54 us  [local_step(): pl.pallas_call(unpack, name='unpack', out_shape=(jax.ShapeDtypeStruct((1,...]
    pallas_call x1 -> x0, local copies, waits for them, and re-layouts: 1.52 us -> none  [local_step(): pl.pallas_call(functools.partial(kernel, axis, rows), name='gcn_step', ou...]
where the time goes in v2:
time: 111 us
  Pallas kernels  110 us (99%)
    pallas_call x1, Pallas kernels, local_step(): pl.pallas_call(functools.partial(kernel, axis, rows), name='gcn_step', ou...  109 us

profile of v2, /device:TPU:0, one launch (start us, length us, event | category | flops | bytes accessed | tf_op | source)
XLA Modules:
  0.0 110.8 jit_solution(8811936267117357887)
XLA Ops:
  0.6 108.6 %gcn_step.1.packed = f32[176,128]{1,0:T(8,128)} custom-call(bf16[512,16384]{1,0:T(8,128)(2,1)} %a_hbm.1, bf16[512,128]{1,0:T(8,128)(2,1)} %x_hbm.1, f32[128,128]{1,0:T(8,128)} %w1_ref.1, f32[40,128]{1,0:T(8,128)} %bitcast.4, s32[1,512]{1,0:T(1,128)} %bitcast.5, s32[4,128]{1,0:T(4,128)} %bitcast.6), custom_call_target="tpu_custom_call" | custom-call | tf_op jit(solution)/shard_map/gcn_step/pallas_call | solution.py:412
  109.3 1.5 %unpack.1 = (f32[1]{0:T(128)}, f32[128,128]{1,0:T(8,128)}, f32[40,128]{1,0:T(8,128)}) custom-call(f32[176,128]{1,0:T(8,128)} %gcn_step.1.packed), custom_call_target="tpu_custom_call" | custom-call | tf_op jit(solution)/shard_map/unpack/pallas_call | solution.py:432

commit v3 on v2

--- a/solution.py
+++ b/solution.py
@@ -11,7 +11,6 @@
 F32 = jnp.float32
 BF16 = jnp.bfloat16
 NDEV = 32
-HALVES = 2
 F = 128
 K = 40
 KP = 48
@@ -27,6 +26,19 @@
 )
 PIECES = 3
 BATCH = 4
+
+CALC, DIAG, XSIDE, YSIDE, LINE, BACK, BDIAG, BX, BY, BEND = range(10)
+CUTS = (0, 48, 96, 128)
+REDUCE_END = (
+    1, 367, 83, 66, 365, 366, 67, 81, 82, 2, 147, 359, 65, 211, 130, 210, 131, 145, 363, 3, 362, 64, 355, 146,
+    358, 80, 354, 195, 364, 275, 194, 357, 208, 361, 356, 193, 416, 129, 144, 209, 259, 258, 192, 480, 360, 274, 353, 128,
+    352, 544, 257, 273, 608, 272, 256,
+)
+REDUCE_MID = (
+    1, 83, 82, 81, 80, 64, 66, 67, 2, 367, 211, 65, 209, 366, 365, 147, 359, 363, 144, 3, 362, 355, 193, 145,
+    357, 361, 130, 195, 354, 358, 194, 131, 210, 364, 416, 208, 353, 275, 356, 129, 146, 480, 259, 273, 192, 258, 360, 257,
+    128, 544, 274, 256, 352, 608, 272,
+)
 
 
 def program(order):
@@ -45,10 +57,10 @@
 
 
 def kernel(axis, rows, a_hbm, x_hbm, w1_ref, w2_ref, lab_ref, mask_ref, out_ref,
-           a_v, xall, hall, acc, s1, s1t, z1t, w2p, ut, mrow, sq,
-           own, outbox, pairin, xin, yin, zin, sums,
+           a_v, xall, hall, acc, s1, s1t, z1t, w2p, w2b, ut, mrow, cnt, sq,
+           own, outbox, pairin, xin, yin, zin, zinb,
            ar1_src, ar1_pin, ar1_pl, ar1_zz, ar1_fin, ar2_src, ar2_pin, ar2_pl, ar2_zz, ar2_fin,
-           a_sem, x_sem, ag1_r, ag1_s, ag2_r, ag2_s, rs_ps, rs_pr, rs_xs, rs_xr, rs_ys, rs_yr, rs_zs, rs_zr,
+           a_sem, x_sem, ag1_r, ag1_s, ag2_r, ag2_s, rs_ps, rs_pr, rs_s, rs_xr, rs_yr, rs_zr, rs_br,
            ar1_s, ar1_r, ar2_s, ar2_r):
     me = lax.axis_index(axis)
     core = me % 2
@@ -99,6 +111,7 @@
     xall[me, rows:rows + TAIL, :] = mrow[...].astype(BF16)
     w2p[...] = jnp.zeros_like(w2p)
     w2p[0:K, :] = w2_ref[...]
+    w2b[...] = w2p[...].T.astype(BF16)
     w1b = w1_ref[...].astype(BF16)
     acc[...] = jnp.zeros_like(acc)
     x_copy.wait()
@@ -112,7 +125,7 @@
             out = jnp.where(i == k, values[k], out)
         return out
 
-    def gather(buf, cuts, r_sem, s_sem, first):
+    def gather(buf, cuts, r_sem, s_sem, first, between_sends=None):
         def piece(b, c):
             return buf.at[b, pl.ds(cuts[c], cuts[c + 1] - cuts[c])]
 
@@ -153,10 +166,16 @@
             lax.fori_loop(0, len(ids), body, 0)
 
         def run(order, between, pending):
+            own_left = PIECES
             for step in program(order):
                 if len(step) == 2:
                     multiply(*step)
                     continue
+                own_left -= step[1:] == (0, 0)
+                if step[1:] != (0, 0) and own_left == 0:
+                    own_left = -1
+                    if between_sends is not None:
+                        between_sends()
                 c, q, j = step
                 b = blocks[q, j, 0]
                 if (q, j) != (0, 0):
@@ -195,14 +214,18 @@
     sq[...] = z1
     acc[...] = jnp.zeros_like(acc)
 
-    drain2 = gather(hall, cuts2, ag2_r, ag2_s, False)
-
-    w2b = w2p[...].T.astype(BF16)
-    w2t = w2p[0:KP, :].astype(BF16)
-
     def count_body(b, tot):
         return tot + xall[b, rows:rows + TAIL, :].astype(F32)
-    label_count = jnp.sum(lax.fori_loop(0, NDEV, count_body, jnp.zeros((TAIL, 128), F32)))
+
+    def early():
+        z1t[...] = sq[...].T
+        s1t[...] = s1[...].astype(F32).T.astype(BF16)
+        cnt[...] = lax.fori_loop(0, NDEV, count_body, jnp.zeros((TAIL, 128), F32))
+
+    drain2 = gather(hall, cuts2, ag2_r, ag2_s, False, early)
+
+    w2t = w2p[0:KP, :].astype(BF16)
+    label_count = jnp.sum(cnt[...])
     s2b = acc[...].astype(BF16)
     z2 = lax.dot_general(w2t, s2b, (((1,), (1,)), ((), ())), preferred_element_type=F32)
     row_id = lax.broadcasted_iota(jnp.int32, (KP, rows), 0)
@@ -228,41 +251,51 @@
 
     def make_ar(src, pin, pl4, zz, fin, s_sem, r_sem):
         n = src.shape[0] // 2
-        sends = []
-
-        def go(c):
-            c.start()
-            sends.append(c)
+
+        def give():
+            lo = pl.multiple_of((1 - core) * n, n)
+            return [rcopy(src.at[pl.ds(lo, n)], pin, s_sem.at[0], r_sem.at[0], pn)]
+
+        def over_plane():
+            return [rcopy(pl4.at[plane], pl4.at[plane], s_sem.at[1 + k], r_sem.at[1 + plane], to)
+                    for k, to in enumerate((xn, yn, dn))]
+
+        def over_line():
+            return [rcopy(zz.at[z], zz.at[z], s_sem.at[4 + k], r_sem.at[5 + z], to) for k, to in enumerate(zothers)]
+
+        def back():
+            return [rcopy(fin.at[core], fin.at[core], s_sem.at[7], r_sem.at[9], pn)]
+
+        def start(copies):
+            for c in copies:
+                c.start()
 
         def s1():
-            lo = pl.multiple_of((1 - core) * n, n)
-            go(rcopy(src.at[pl.ds(lo, n)], pin, s_sem.at[0], r_sem.at[0], pn))
+            start(give())
 
         def s2():
             rcopy(pin, pin, s_sem.at[0], r_sem.at[0], pn).wait_recv()
             lo = pl.multiple_of(core * n, n)
             pl4[plane] = src[pl.ds(lo, n), :] + pin[...]
-            for k, to in enumerate((xn, yn, dn)):
-                go(rcopy(pl4.at[plane], pl4.at[plane], s_sem.at[1 + k], r_sem.at[1 + plane], to))
+            start(over_plane())
 
         def s3():
             for px, py in ((1, 0), (0, 1), (1, 1)):
                 p = (y + py * (1 - 2 * y)) * 2 + x + px * (1 - 2 * x)
                 rcopy(pl4.at[p], pl4.at[p], s_sem.at[0], r_sem.at[1 + p], pn).wait_recv()
             zz[z] = (pl4[0] + pl4[1]) + (pl4[2] + pl4[3])
-            for k, to in enumerate(zothers):
-                go(rcopy(zz.at[z], zz.at[z], s_sem.at[4 + k], r_sem.at[5 + z], to))
+            start(over_line())
 
         def s4():
             for k in (1, 2, 3):
                 o = (z + k) % 4
                 rcopy(zz.at[o], zz.at[o], s_sem.at[0], r_sem.at[5 + o], pn).wait_recv()
             fin[core] = (zz[0] + zz[1]) + (zz[2] + zz[3])
-            go(rcopy(fin.at[core], fin.at[core], s_sem.at[7], r_sem.at[9], pn))
+            start(back())
 
         def s5():
             rcopy(fin.at[1 - core], fin.at[1 - core], s_sem.at[0], r_sem.at[9], pn).wait_recv()
-            for c in sends:
+            for c in give() + over_plane() + over_line() + back():
                 c.wait_send()
 
         return s1, s2, s3, s4, s5
@@ -288,87 +321,113 @@
         parts(0, 3 - k)
         return carry
 
-    fh = F // HALVES
-
-    def hs(h):
-        return pl.ds(h * fh, fh)
-
-    def pair_add(q, j):
-        i = q * 4 + j
-        rcopy(pairin.at[i], pairin.at[i], rs_ps.at[0], rs_pr.at[i], pn).wait_recv()
-        own[i] = own[i] + pairin[i]
-
-    def xslot(q, j):
-        return 2 + j if q == 0 else (3 - j) // 2
-
-    rs_sends = []
-
-    def rs_send(src, dst, s_arr, r_arr, k, h, dk, to):
-        c = rcopy(src, dst, s_arr.at[k, h], r_arr.at[dk, h], to)
-        c.start()
-        rs_sends.append(c)
-
-    lax.fori_loop(0, 4, diag_body, 0)
-    for j in (3, 2, 1, 0):
-        pair_add(3, j)
-        for h in range(HALVES):
-            if j % 2 == 1:
-                s = xslot(2, j)
-                rs_send(own.at[12 + j, hs(h)], xin.at[s, hs(h)], rs_xs, rs_xr, s, h, s, xn)
+    def piece_rows(c):
+        return pl.ds(CUTS[c], CUTS[c + 1] - CUTS[c])
+
+    def landed(ref, sem):
+        rcopy(ref, ref, rs_s.at[0], sem, pn).wait_recv()
+
+    to_line = zin_n + mid * (zout_n - zin_n)
+    mid_slot = {3: 3, 2: 2, 1: 5, 0: 0}
+    line_slot = {3: 3 + 2 * mid, 2: 2 + 2 * mid, 1: 4 * mid}
+    line_to = {3: zin_n, 2: zin_n, 1: to_line}
+
+    def reduce_copy(k, i, c, dst, slot, r_sem, r_slot, to):
+        target = dst.at[slot] if dst is zinb else dst.at[slot, piece_rows(c)]
+        return rcopy(own.at[i, piece_rows(c)], target, rs_s.at[k], r_sem.at[r_slot], to)
+
+    def reduce(order, between, sent):
+        added = set()
+
+        def value(q, j):
+            i = q * 4 + j
+            if i not in added:
+                added.add(i)
+                rcopy(pairin.at[i], pairin.at[i], rs_ps.at[0], rs_pr.at[i], pn).wait_recv()
+                own[i] = own[i] + pairin[i]
+            return i
+
+        def send(i, dst, slot, r_sem, r_slot, to):
+            sent.append((i, c, dst, slot, r_sem, r_slot, to))
+            reduce_copy(len(sent) - 1, *sent[-1]).start()
+
+        for code in order:
+            kind, c, q, j = code // 64, code // 16 % 4, code // 4 % 4, code % 4
+            if kind == CALC:
+                if j == 1:
+                    lax.fori_loop(0, 4, diag_body, 0)
+                elif j == 2:
+                    lax.fori_loop(0, 8, side_body, 0)
+                    small[1]()
+                else:
+                    lax.fori_loop(0, 4, own_body, 0)
+                continue
+            hs = piece_rows(c)
+            diag = (3 - j) // 2
+            if kind == DIAG:
+                i = value(3, j)
+                if j % 2 == 1:
+                    send(i, xin, diag, rs_xr, (diag, c), xn)
+                else:
+                    send(i, yin, diag, rs_yr, (diag, c), yn)
+            elif kind == XSIDE:
+                i = value(1, j)
+                if j % 2 == 0:
+                    landed(yin.at[diag, hs], rs_yr.at[diag, c])
+                    own[i, hs] = own[i, hs] + yin[diag, hs]
+                send(i, xin, 2 + j, rs_xr, (2 + j, c), xn)
+            elif kind == YSIDE:
+                i = value(2, j)
+                if j % 2 == 1:
+                    landed(xin.at[diag, hs], rs_xr.at[diag, c])
+                    own[i, hs] = own[i, hs] + xin[diag, hs]
+                send(i, yin, 2 + j, rs_yr, (2 + j, c), yn)
+            elif kind == LINE:
+                i = value(0, j)
+                landed(xin.at[2 + j, hs], rs_xr.at[2 + j, c])
+                landed(yin.at[2 + j, hs], rs_yr.at[2 + j, c])
+                own[i, hs] = (own[i, hs] + xin[2 + j, hs]) + yin[2 + j, hs]
+                for t in ([mid_slot[j]] if between else []) + ([4] if j == 0 else []):
+                    landed(zin.at[t, hs], rs_zr.at[t, c])
+                    own[i, hs] = own[i, hs] + zin[t, hs]
+                if j > 0:
+                    send(i, zin, line_slot[j], rs_zr, (line_slot[j], c), line_to[j])
+            elif kind == BACK:
+                i = value(q, j)
+                for t in ([mid_slot[j]] if between else []) + ([4] if j == 0 else []):
+                    landed(zinb.at[q, t], rs_br.at[q, t])
+                    own[i, hs] = own[i, hs] + zinb[q, t]
+                if j > 0:
+                    send(i, zinb, (q, line_slot[j]), rs_br, (q, line_slot[j]), line_to[j])
+            elif kind == BDIAG:
+                send(12, xin, 0, rs_xr, (0, c), xn)
+            elif kind == BX:
+                send(4, xin, 2, rs_xr, (2, c), xn)
+            elif kind == BY:
+                landed(xin.at[0, hs], rs_xr.at[0, c])
+                own[8, hs] = own[8, hs] + xin[0, hs]
+                send(8, yin, 2, rs_yr, (2, c), yn)
             else:
-                s = xslot(1, j)
-                rs_send(own.at[12 + j, hs(h)], yin.at[s, hs(h)], rs_ys, rs_yr, s, h, s, yn)
-    lax.fori_loop(0, 8, side_body, 0)
-    small[1]()
-    lax.fori_loop(0, 4, own_body, 0)
-    for j in (3, 2, 1, 0):
-        pair_add(1, j)
-        pair_add(2, j)
-    for j in (3, 2, 1, 0):
-        for h in range(HALVES):
-            ix, iy = 4 + j, 8 + j
-            if j % 2 == 1:
-                s = xslot(2, j)
-                rcopy(xin.at[s, hs(h)], xin.at[s, hs(h)], rs_xs.at[0, 0], rs_xr.at[s, h], pn).wait_recv()
-                own[iy, hs(h)] = own[iy, hs(h)] + xin[s, hs(h)]
-            else:
-                s = xslot(1, j)
-                rcopy(yin.at[s, hs(h)], yin.at[s, hs(h)], rs_ys.at[0, 0], rs_yr.at[s, h], pn).wait_recv()
-                own[ix, hs(h)] = own[ix, hs(h)] + yin[s, hs(h)]
-            rs_send(own.at[ix, hs(h)], xin.at[2 + j, hs(h)], rs_xs, rs_xr, 2 + j, h, 2 + j, xn)
-            rs_send(own.at[iy, hs(h)], yin.at[2 + j, hs(h)], rs_ys, rs_yr, 2 + j, h, 2 + j, yn)
-    for j in (3, 2, 1, 0):
-        pair_add(0, j)
-    small[2]()
-
-    z1t[...] = sq[...].T
-    s1t[...] = s1[...].astype(F32).T.astype(BF16)
-
-    def z_wait(s, h):
-        rcopy(zin.at[s, hs(h)], zin.at[s, hs(h)], rs_zs.at[0, 0], rs_zr.at[s, h], pn).wait_recv()
-
-    for j in (3, 2, 1, 0):
-        for h in range(HALVES):
-            for arr, r_arr in ((xin, rs_xr), (yin, rs_yr)):
-                rcopy(arr.at[2 + j, hs(h)], arr.at[2 + j, hs(h)], rs_xs.at[0, 0], r_arr.at[2 + j, h], pn).wait_recv()
-            sums[j, hs(h)] = (own[j, hs(h)] + xin[2 + j, hs(h)]) + yin[2 + j, hs(h)]
-
-            @pl.when(mid == 1)
-            def _():
-                s = {3: 3, 2: 2, 1: 5, 0: 0}[j]
-                z_wait(s, h)
-                sums[j, hs(h)] = sums[j, hs(h)] + zin[s, hs(h)]
-            if j > 0:
-                to = zin_n if j > 1 else dev(x, y, z_in + mid * (z_out - z_in), core)
-                slot = j + 2 * mid if j > 1 else 4 * mid
-                rs_send(sums.at[j, hs(h)], zin.at[slot, hs(h)], rs_zs, rs_zr, j, h, slot, to)
-            else:
-                z_wait(4, h)
-                sums[0, hs(h)] = sums[0, hs(h)] + zin[4, hs(h)]
-        if j == 3:
-            small[3]()
-
-    g1t = jnp.where(z1t[...] > 0.0, sums[0], 0.0).astype(BF16)
+                landed(xin.at[2, hs], rs_xr.at[2, c])
+                landed(yin.at[2, hs], rs_yr.at[2, c])
+                own[0, hs] = (own[0, hs] + xin[2, hs]) + yin[2, hs]
+            steps_left = len(order) - 1 - order.index(code)
+            if steps_left == 24:
+                small[2]()
+            elif steps_left == 6:
+                small[3]()
+
+    reduced = {True: [], False: []}
+
+    @pl.when(is_mid)
+    def _():
+        reduce(REDUCE_MID, True, reduced[True])
+
+    @pl.when(mid == 0)
+    def _():
+        reduce(REDUCE_END, False, reduced[False])
+
+    g1t = jnp.where(z1t[...] > 0.0, own[0], 0.0).astype(BF16)
     ar1_src[...] = lax.dot_general(s1t[...], g1t, (((1,), (1,)), ((), ())), preferred_element_type=F32)
     big = make_ar(ar1_src, ar1_pin, ar1_pl, ar1_zz, ar1_fin, ar1_s, ar1_r)
     big[0]()
@@ -381,8 +440,11 @@
     drain1()
     drain2()
     big[2]()
-    for c in rs_sends:
-        c.wait_send()
+    for between, when in ((True, is_mid), (False, mid == 0)):
+        @pl.when(when)
+        def _():
+            for k, spec in enumerate(reduced[between]):
+                reduce_copy(k, *spec).wait_send()
     for i in range(16):
         rcopy(outbox.at[i], pairin.at[i], rs_ps.at[i], rs_pr.at[i], pn).wait_send()
     big[3]()
@@ -419,12 +481,13 @@
                 pltpu.VMEM((NDEV, rows, rows), BF16), pltpu.VMEM((NDEV, rows + TAIL, F), BF16),
                 pltpu.VMEM((NDEV, rows, F), BF16), pltpu.VMEM((rows, F), F32), pltpu.VMEM((rows, F), BF16),
                 pltpu.VMEM((F, rows), BF16), pltpu.VMEM((F, rows), F32), pltpu.VMEM((F, F), F32),
-                pltpu.VMEM((F, rows), BF16), pltpu.VMEM((TAIL, F), F32), pltpu.VMEM((rows, F), F32),
-                blk(16), blk(16), blk(16), blk(6), blk(6), blk(6), blk(4),
+                pltpu.VMEM((F, F), BF16), pltpu.VMEM((F, rows), BF16), pltpu.VMEM((TAIL, F), F32), pltpu.VMEM((TAIL, F), F32),
+                pltpu.VMEM((rows, F), F32),
+                blk(16), blk(16), blk(16), blk(6), blk(6), blk(6),
+                pltpu.VMEM((4, 6, F - CUTS[-2], rows), F32),
                 *ar(F // 2), *ar(KP // 2),
                 dma((NDEV,)), dma(()), dma((NDEV, PIECES)), dma((nsend,)), dma((NDEV, PIECES)), dma((nsend,)),
-                dma((16,)), dma((16,)), dma((6, HALVES)), dma((6, HALVES)), dma((6, HALVES)), dma((6, HALVES)),
-                dma((6, HALVES)), dma((6, HALVES)), dma((8,)), dma((10,)), dma((8,)), dma((10,)),
+                dma((16,)), dma((16,)), dma((64,)), dma((6, 3)), dma((6, 3)), dma((6, 3)), dma((4, 6)), dma((8,)), dma((10,)), dma((8,)), dma((10,)),
             ],
             compiler_params=pltpu.CompilerParams(collective_id=0, has_side_effects=True,
                                                  vmem_limit_bytes=60 * 1024 * 1024),

time: 111 us -> 107 us (0.964)
  Pallas kernels: 110 us -> 106 us
    pallas_call x1, Pallas kernels: 109 us -> 105 us  [local_step(): pl.pallas_call(functools.partial(kernel, axis, rows), name='gcn_step', ou...]
where the time goes in v3:
time: 107 us
  Pallas kernels  106 us (99%)
    pallas_call x1, Pallas kernels, local_step(): pl.pallas_call(functools.partial(kernel, axis, rows), name='gcn_step', ou...  105 us

profile of v3, /device:TPU:0, one launch (start us, length us, event | category | flops | bytes accessed | tf_op | source)
XLA Modules:
  0.0 107.0 jit_solution(1191856441636067074)
XLA Ops:
  0.6 104.9 %gcn_step.1.packed = f32[176,128]{1,0:T(8,128)} custom-call(bf16[512,16384]{1,0:T(8,128)(2,1)} %a_hbm.1, bf16[512,128]{1,0:T(8,128)(2,1)} %x_hbm.1, f32[128,128]{1,0:T(8,128)} %w1_ref.1, f32[40,128]{1,0:T(8,128)} %bitcast.4, s32[1,512]{1,0:T(1,128)} %bitcast.5, s32[4,128]{1,0:T(4,128)} %bitcast.6), custom_call_target="tpu_custom_call" | custom-call | tf_op jit(solution)/shard_map/gcn_step/pallas_call | solution.py:474
  105.5 1.5 %unpack.1 = (f32[1]{0:T(128)}, f32[128,128]{1,0:T(8,128)}, f32[40,128]{1,0:T(8,128)}) custom-call(f32[176,128]{1,0:T(8,128)} %gcn_step.1.packed), custom_call_target="tpu_custom_call" | custom-call | tf_op jit(solution)/shard_map/unpack/pallas_call | solution.py:495

commit v4 on v3

--- a/solution.py
+++ b/solution.py
@@ -17,27 +17,27 @@
 TAIL = 16
 
 ORDER_END = (
-    0, 16, 32, 1, 17, 40, 8, 2, 36, 5, 18, 21, 33, 44, 37, 24, 3, 12, 19, 34, 38, 10, 22, 28,
-    29, 13, 26, 4, 7, 9, 6, 45, 23, 43, 41, 42, 11, 20, 39, 27, 25, 15, 30, 14, 46, 35, 47, 31,
+    0, 32, 16, 8, 36, 40, 17, 33, 1, 12, 2, 44, 4, 25, 21, 24, 5, 18, 9, 3, 6, 37, 19, 20,
+    10, 28, 41, 22, 45, 26, 7, 43, 34, 23, 42, 39, 13, 29, 11, 35, 15, 38, 14, 27, 30, 46, 47, 31,
 )
 ORDER_MID = (
-    0, 16, 32, 2, 1, 18, 17, 36, 40, 3, 19, 10, 41, 26, 24, 34, 5, 38, 37, 42, 21, 44, 33, 4,
-    43, 11, 20, 7, 45, 39, 8, 23, 9, 46, 27, 35, 22, 47, 14, 25, 30, 6, 15, 31, 13, 28, 29, 12,
+    0, 16, 32, 1, 2, 18, 36, 34, 40, 5, 17, 9, 3, 37, 41, 33, 42, 19, 45, 39, 8, 10, 24, 44,
+    4, 20, 21, 7, 11, 43, 47, 27, 35, 38, 23, 46, 22, 25, 29, 26, 12, 6, 15, 13, 31, 14, 28, 30,
 )
 PIECES = 3
 BATCH = 4
 
 CALC, DIAG, XSIDE, YSIDE, LINE, BACK, BDIAG, BX, BY, BEND = range(10)
-CUTS = (0, 48, 96, 128)
+CUTS = (0, 56, 104, 128)
 REDUCE_END = (
-    1, 367, 83, 66, 365, 366, 67, 81, 82, 2, 147, 359, 65, 211, 130, 210, 131, 145, 363, 3, 362, 64, 355, 146,
-    358, 80, 354, 195, 364, 275, 194, 357, 208, 361, 356, 193, 416, 129, 144, 209, 259, 258, 192, 480, 360, 274, 353, 128,
-    352, 544, 257, 273, 608, 272, 256,
+    1, 67, 367, 66, 366, 81, 365, 82, 2, 362, 83, 195, 363, 358, 131, 359, 64, 65, 146, 361, 3, 355, 194, 210,
+    211, 354, 353, 147, 357, 193, 80, 209, 145, 130, 259, 364, 128, 274, 129, 275, 258, 416, 356, 144, 192, 273, 360, 352,
+    208, 257, 544, 480, 272, 256, 608,
 )
 REDUCE_MID = (
-    1, 83, 82, 81, 80, 64, 66, 67, 2, 367, 211, 65, 209, 366, 365, 147, 359, 363, 144, 3, 362, 355, 193, 145,
-    357, 361, 130, 195, 354, 358, 194, 131, 210, 364, 416, 208, 353, 275, 356, 129, 146, 480, 259, 273, 192, 258, 360, 257,
-    128, 544, 274, 256, 352, 608, 272,
+    1, 67, 82, 81, 64, 83, 2, 66, 131, 366, 65, 367, 80, 195, 362, 363, 210, 147, 358, 361, 364, 365, 3, 359,
+    355, 211, 130, 354, 353, 193, 194, 146, 356, 145, 129, 259, 416, 144, 357, 209, 360, 128, 274, 480, 208, 275, 257, 192,
+    273, 258, 352, 544, 272, 256, 608,
 )
 
 
@@ -203,8 +203,8 @@
                         rcopy(piece(b, c), piece(b, c), s_sem.at[k], r_sem.at[b, c], to).wait_send()
         return drain
 
-    cuts1 = (0, rows * 3 // 8, rows * 6 // 8, rows + TAIL)
-    cuts2 = (0, rows * 3 // 8, rows * 6 // 8, rows)
+    cuts1 = (0, rows * 13 // 32, rows * 26 // 32, rows + TAIL)
+    cuts2 = (0, rows * 13 // 32, rows * 26 // 32, rows)
     drain1 = gather(xall, cuts1, ag1_r, ag1_s, True)
 
     s1b = acc[...].astype(BF16)
@@ -474,7 +474,7 @@
         packed = pl.pallas_call(
             functools.partial(kernel, axis, rows),
             name='gcn_step',
-            out_shape=jax.ShapeDtypeStruct((F + KP, F), F32),
+            out_shape=pltpu.VMEM((F + KP, F), F32),
             in_specs=[hbm, hbm, vmem, vmem, vmem, vmem],
             out_specs=vmem,
             scratch_shapes=[
@@ -499,7 +499,7 @@
                        jax.ShapeDtypeStruct((K, F), F32)),
             in_specs=[vmem],
             out_specs=(pl.BlockSpec(memory_space=pltpu.SMEM), vmem, vmem),
-        )(packed)
+        )(pltpu.with_memory_space_constraint(packed, pltpu.VMEM))
         return loss, dw_one, dw_two_t.T
 
     return jax.shard_map(local_step, mesh=mesh,

time: 107 us -> 111 us (1.037)
  Pallas kernels: 106 us -> 111 us
    pallas_call x1, Pallas kernels: 105 us -> 110 us  [local_step(): pl.pallas_call(functools.partial(kernel, axis, rows), name='gcn_step', ou...]
where the time goes in v4:
time: 111 us
  Pallas kernels  111 us (100%)
    pallas_call x1, Pallas kernels, local_step(): pl.pallas_call(functools.partial(kernel, axis, rows), name='gcn_step', ou...  110 us

profile of v4, /device:TPU:0, one launch (start us, length us, event | category | flops | bytes accessed | tf_op | source)
XLA Modules:
  0.0 111.2 jit_solution(4989657081934702913)
XLA Ops:
  0.6 109.9 %gcn_step.1.packed = f32[176,128]{1,0:T(8,128)S(1)} custom-call(bf16[512,16384]{1,0:T(8,128)(2,1)} %a_hbm.1, bf16[512,128]{1,0:T(8,128)(2,1)} %x_hbm.1, f32[128,128]{1,0:T(8,128)} %w1_ref.1, f32[40,128]{1,0:T(8,128)} %bitcast.4, s32[1,512]{1,0:T(1,128)} %bitcast.5, s32[4,128]{1,0:T(4,128)} %bitcast.6), custom_call_target="tpu_custom_call" | custom-call | tf_op jit(solution)/shard_map/gcn_step/pallas_call | solution.py:474
  110.5 0.6 unpack.1

commit v5 on v3

--- a/solution.py
+++ b/solution.py
@@ -28,16 +28,16 @@
 BATCH = 4
 
 CALC, DIAG, XSIDE, YSIDE, LINE, BACK, BDIAG, BX, BY, BEND = range(10)
-CUTS = (0, 48, 96, 128)
+CUTS = (0, 56, 104, 128)
 REDUCE_END = (
-    1, 367, 83, 66, 365, 366, 67, 81, 82, 2, 147, 359, 65, 211, 130, 210, 131, 145, 363, 3, 362, 64, 355, 146,
-    358, 80, 354, 195, 364, 275, 194, 357, 208, 361, 356, 193, 416, 129, 144, 209, 259, 258, 192, 480, 360, 274, 353, 128,
-    352, 544, 257, 273, 608, 272, 256,
+    1, 83, 82, 367, 66, 366, 67, 2, 362, 210, 81, 363, 358, 131, 146, 211, 3, 147, 359, 195, 357, 354, 365, 65,
+    194, 355, 130, 145, 364, 64, 361, 353, 259, 275, 209, 80, 416, 129, 193, 208, 274, 258, 128, 273, 352, 356, 144, 480,
+    360, 192, 257, 544, 256, 272, 608,
 )
 REDUCE_MID = (
-    1, 83, 82, 81, 80, 64, 66, 67, 2, 367, 211, 65, 209, 366, 365, 147, 359, 363, 144, 3, 362, 355, 193, 145,
-    357, 361, 130, 195, 354, 358, 194, 131, 210, 364, 416, 208, 353, 275, 356, 129, 146, 480, 259, 273, 192, 258, 360, 257,
-    128, 544, 274, 256, 352, 608, 272,
+    1, 83, 67, 82, 64, 2, 147, 367, 65, 66, 366, 80, 362, 365, 211, 195, 363, 146, 81, 358, 359, 3, 354, 210,
+    361, 131, 357, 364, 355, 416, 193, 360, 145, 353, 194, 129, 209, 259, 544, 356, 208, 130, 128, 275, 274, 352, 144, 192,
+    480, 257, 273, 258, 272, 256, 608,
 )
 
 
@@ -474,7 +474,7 @@
         packed = pl.pallas_call(
             functools.partial(kernel, axis, rows),
             name='gcn_step',
-            out_shape=jax.ShapeDtypeStruct((F + KP, F), F32),
+            out_shape=pltpu.VMEM((F + KP, F), F32),
             in_specs=[hbm, hbm, vmem, vmem, vmem, vmem],
             out_specs=vmem,
             scratch_shapes=[
@@ -499,7 +499,7 @@
                        jax.ShapeDtypeStruct((K, F), F32)),
             in_specs=[vmem],
             out_specs=(pl.BlockSpec(memory_space=pltpu.SMEM), vmem, vmem),
-        )(packed)
+        )(pltpu.with_memory_space_constraint(packed, pltpu.VMEM))
         return loss, dw_one, dw_two_t.T
 
     return jax.shard_map(local_step, mesh=mesh,

time: 107 us -> 106 us (level)
  no operation moved by 1% of the time
where the time goes in v5:
time: 106 us; the launch traced here: 105 us
  Pallas kernels  105 us (99%)
    pallas_call x1, Pallas kernels, local_step(): pl.pallas_call(functools.partial(kernel, axis, rows), name='gcn_step', ou...  104 us

profile of v5, /device:TPU:0, one launch (start us, length us, event | category | flops | bytes accessed | tf_op | source)
XLA Modules:
  0.0 105.4 jit_solution(2233901684124967611)
XLA Ops:
  0.6 104.1 %gcn_step.1.packed = f32[176,128]{1,0:T(8,128)S(1)} custom-call(bf16[512,16384]{1,0:T(8,128)(2,1)} %a_hbm.1, bf16[512,128]{1,0:T(8,128)(2,1)} %x_hbm.1, f32[128,128]{1,0:T(8,128)} %w1_ref.1, f32[40,128]{1,0:T(8,128)} %bitcast.4, s32[1,512]{1,0:T(1,128)} %bitcast.5, s32[4,128]{1,0:T(4,128)} %bitcast.6), custom_call_target="tpu_custom_call" | custom-call | tf_op jit(solution)/shard_map/gcn_step/pallas_call | solution.py:474
  104.7 0.6 unpack.1

commit v6 on v5

--- a/solution.py
+++ b/solution.py
@@ -56,7 +56,8 @@
     return steps + [(ready, late), ([], following)]
 
 
-def kernel(axis, rows, a_hbm, x_hbm, w1_ref, w2_ref, lab_ref, mask_ref, out_ref,
+def kernel(axis, rows, a_hbm, x_hbm, w1_hbm, w2_hbm, lab_hbm, mask_hbm, out_ref,
+           w1_v, lab_v, mask_v, p_sem,
            a_v, xall, hall, acc, s1, s1t, z1t, w2p, w2b, ut, mrow, cnt, sq,
            own, outbox, pairin, xin, yin, zin, zinb,
            ar1_src, ar1_pin, ar1_pl, ar1_zz, ar1_fin, ar2_src, ar2_pin, ar2_pl, ar2_zz, ar2_fin,
@@ -100,20 +101,25 @@
 
     x_copy = pltpu.make_async_copy(x_hbm, xall.at[me, pl.ds(0, rows)], x_sem)
     x_copy.start()
+    mask_copy = pltpu.make_async_copy(mask_hbm, mask_v, p_sem.at[0])
+    mask_copy.start()
+    barrier = pltpu.get_barrier_semaphore()
+    for to in [pn, xn, yn, dn] + zothers:
+        pl.semaphore_signal(barrier, inc=1, device_id=(to,), device_id_type=MESH)
     blocks = {(q, j, o): bid(q, j, o) for q in range(4) for j in range(4) for o in range(2)}
     for b in blocks.values():
         a_copy(b).start()
-    barrier = pltpu.get_barrier_semaphore()
-    for to in [pn, xn, yn, dn] + zothers:
-        pl.semaphore_signal(barrier, inc=1, device_id=(to,), device_id_type=MESH)
+    w1_copy = pltpu.make_async_copy(w1_hbm, w1_v, p_sem.at[1])
+    w2_copy = pltpu.make_async_copy(w2_hbm, w2p.at[pl.ds(0, K)], p_sem.at[2])
+    lab_copy = pltpu.make_async_copy(lab_hbm, lab_v, p_sem.at[3])
+    for copy in (w1_copy, w2_copy, lab_copy):
+        copy.start()
     mrow[...] = jnp.zeros_like(mrow)
-    mrow[0:rows // 128, :] = mask_ref[...].astype(F32)
+    w2p[K:F, :] = jnp.zeros((F - K, F), F32)
+    acc[...] = jnp.zeros_like(acc)
+    mask_copy.wait()
+    mrow[0:rows // 128, :] = mask_v[...].astype(F32)
     xall[me, rows:rows + TAIL, :] = mrow[...].astype(BF16)
-    w2p[...] = jnp.zeros_like(w2p)
-    w2p[0:K, :] = w2_ref[...]
-    w2b[...] = w2p[...].T.astype(BF16)
-    w1b = w1_ref[...].astype(BF16)
-    acc[...] = jnp.zeros_like(acc)
     x_copy.wait()
     pl.semaphore_wait(barrier, 7)
 
@@ -209,7 +215,8 @@
 
     s1b = acc[...].astype(BF16)
     s1[...] = s1b
-    z1 = jnp.dot(s1b, w1b, preferred_element_type=F32)
+    w1_copy.wait()
+    z1 = jnp.dot(s1b, w1_v[...].astype(BF16), preferred_element_type=F32)
     hall[me] = jnp.maximum(z1, 0.0).astype(BF16)
     sq[...] = z1
     acc[...] = jnp.zeros_like(acc)
@@ -218,10 +225,13 @@
         return tot + xall[b, rows:rows + TAIL, :].astype(F32)
 
     def early():
+        w2b[...] = w2p[...].T.astype(BF16)
         z1t[...] = sq[...].T
         s1t[...] = s1[...].astype(F32).T.astype(BF16)
         cnt[...] = lax.fori_loop(0, NDEV, count_body, jnp.zeros((TAIL, 128), F32))
 
+    w2_copy.wait()
+    lab_copy.wait()
     drain2 = gather(hall, cuts2, ag2_r, ag2_s, False, early)
 
     w2t = w2p[0:KP, :].astype(BF16)
@@ -234,7 +244,7 @@
     shifted = jnp.where(valid, z2 - top, 0.0)
     norm = jnp.log(jnp.sum(jnp.where(valid, jnp.exp(shifted), 0.0), axis=0, keepdims=True))
     log_prob = shifted - norm
-    hot = row_id == lab_ref[...]
+    hot = row_id == lab_v[...]
     onehot = jnp.where(hot, 1.0, 0.0)
     weight = jnp.concatenate([mrow[k:k + 1, :] for k in range(rows // 128)], axis=1)
     loss_row = -weight * jnp.sum(jnp.where(hot, log_prob, 0.0), axis=0, keepdims=True)
@@ -470,14 +480,16 @@
         ar = lambda n: [pltpu.VMEM((2 * n, F), F32), pltpu.VMEM((n, F), F32), pltpu.VMEM((4, n, F), F32),
                         pltpu.VMEM((4, n, F), F32), pltpu.VMEM((2, n, F), F32)]
         vmem = pl.BlockSpec(memory_space=pltpu.VMEM)
-        hbm = pl.BlockSpec(memory_space=pl.ANY)
+        hbm = pl.BlockSpec(memory_space=pltpu.HBM)
         packed = pl.pallas_call(
             functools.partial(kernel, axis, rows),
             name='gcn_step',
             out_shape=pltpu.VMEM((F + KP, F), F32),
-            in_specs=[hbm, hbm, vmem, vmem, vmem, vmem],
+            in_specs=[hbm] * 6,
             out_specs=vmem,
             scratch_shapes=[
+                pltpu.VMEM((F, F), F32), pltpu.VMEM((1, rows), jnp.int32), pltpu.VMEM((rows // 128, 128), jnp.int32),
+                dma((4,)),
                 pltpu.VMEM((NDEV, rows, rows), BF16), pltpu.VMEM((NDEV, rows + TAIL, F), BF16),
                 pltpu.VMEM((NDEV, rows, F), BF16), pltpu.VMEM((rows, F), F32), pltpu.VMEM((rows, F), BF16),
                 pltpu.VMEM((F, rows), BF16), pltpu.VMEM((F, rows), F32), pltpu.VMEM((F, F), F32),

time: 106 us -> 100 us (0.943)
  Pallas kernels: 105 us -> 99.5 us
    pallas_call x1, Pallas kernels: 104 us -> 98.9 us  [local_step(): pl.pallas_call(functools.partial(kernel, axis, rows), name='gcn_step', ou...]
where the time goes in v6:
time: 100 us
  Pallas kernels  99.5 us (100%)
    pallas_call x1, Pallas kernels, local_step(): pl.pallas_call(functools.partial(kernel, axis, rows), name='gcn_step', ou...  98.9 us

profile of v6, /device:TPU:0, one launch (start us, length us, event | category | flops | bytes accessed | tf_op | source)
XLA Modules:
  0.0 100.2 jit_solution(4357564115131892958)
XLA Ops:
  0.6 98.9 %gcn_step.1.packed = f32[176,128]{1,0:T(8,128)S(1)} custom-call(bf16[512,16384]{1,0:T(8,128)(2,1)} %a_hbm.1, bf16[512,128]{1,0:T(8,128)(2,1)} %x_hbm.1, f32[128,128]{1,0:T(8,128)} %w1_hbm.1, f32[40,128]{1,0:T(8,128)} %bitcast.4, s32[1,512]{1,0:T(1,128)} %bitcast.5, s32[4,128]{1,0:T(4,128)} %bitcast.6), custom_call_target="tpu_custom_call" | custom-call | tf_op jit(solution)/shard_map/gcn_step/pallas_call | solution.py:484
  99.5 0.6 unpack.1
